TPU v7x, 32 devices: a whole 2x2x4 slice. The times are simulated.
32 devices in a mesh: section: 4 (over y, x), expert: 8 (over z, core).
Axes of the slice: x: 2, y: 2, z: 4, core: 2. Of those that a mesh axis runs over, the one named last changes fastest.
Arguments:
- tokens: bfloat16 [8, 64, 2048], P(None, 'expert'), may hold values from -6 to 6
- norm_gain: float32 [2, 2048], replicated, may hold values from 0.1 to 1.9
- w_gate: bfloat16 [4, 2048, 14336], P('section', None, 'expert'), may hold values from -0.125 to 0.125
- w_up: bfloat16 [4, 2048, 14336], P('section', None, 'expert'), may hold values from -0.125 to 0.125
- w_down: bfloat16 [4, 14336, 2048], P('section', 'expert'), may hold values from -0.0625 to 0.0625
- expert_ids: int32 [2, 8, 64, 2], P(None, None, 'expert'), may hold values from 0 to 3, as said below
- slot_ids: int32 [2, 8, 64, 2], P(None, None, 'expert'), may hold values from 0 to 4, as said below
- dropped: int32 [2, 8, 64, 2], P(None, None, 'expert'), may hold values from 0 to 1, as said below
- gate_weights: float32 [2, 8, 64, 2], P(None, None, 'expert'), may hold values from 0.1 to 1
Outputs:
- states: bfloat16 [4, 8, 64, 2048], P('section', None, 'expert')
Inputs may be any that keep to these rules, and one draw needn't show every extreme that they name: `expert_ids`: the two experts of a token differ. `slot_ids`: among the kept choices of the tokens of one index of expert that name one expert, the slots are 0, 1, ... up to their count less one, each once. At most 5 kept choices of the tokens of one index of expert name one expert, and a choice is dropped only where 5 kept choices of its index of expert name its expert; in each layer and micro-batch some expert receives exactly 5 kept choices from every index of expert.
All inputs are finite; a program needn't handle non-finite values.
Results may differ from a plain program's by a relative error of at most 0.025.
Values may be sent and summed in bfloat16 or wider, within the bound.
A program may use at most 64 MiB of HBM per device.

v0:
```python
import jax
import jax.numpy as jnp
from jax import lax
from jax.sharding import PartitionSpec as P

EXPERTS = 4


def shortened(value):
    return jax.tree.map(lambda a: a.astype(jnp.bfloat16) if a.dtype == jnp.float32 else a, value)


def shifted(value, axis, by):
    size = lax.axis_size(axis)
    pairs = [(i, i + by) for i in range(size) if 0 <= i + by < size]
    return lax.ppermute(value, axis, pairs)


def on_device(tokens, norm_gain, w_gate, w_up, w_down, expert_ids, slot_ids, dropped, gate_weights):
    groups = lax.axis_size("expert")
    sections = lax.axis_size("section")
    section_at = lax.axis_index("section")
    local_count = EXPERTS // 2
    shards = groups // local_count
    micro_count, tok_rows, model_width = tokens.shape
    capacity = 5 * tok_rows // (2 * EXPERTS)
    slot_limit = local_count * capacity
    layer_at = section_at // 2
    half_at = section_at % 2
    odd_section = half_at == 1
    gain_row = lax.dynamic_index_in_dim(norm_gain, layer_at, 0, keepdims=False)
    gate_mat = w_gate[0]
    up_mat = w_up[0]
    down_mat = w_down[0]
    route_all = lax.dynamic_index_in_dim(expert_ids, layer_at, 0, keepdims=False)
    slot_all = lax.dynamic_index_in_dim(slot_ids, layer_at, 0, keepdims=False)
    drop_all = lax.dynamic_index_in_dim(dropped, layer_at, 0, keepdims=False)
    weigh_all = lax.dynamic_index_in_dim(gate_weights, layer_at, 0, keepdims=False)

    def expert_rows(received):
        flat_rows = received.reshape(-1, model_width)
        gate_vals = jnp.dot(flat_rows, gate_mat, preferred_element_type=jnp.float32)
        up_vals = jnp.dot(flat_rows, up_mat, preferred_element_type=jnp.float32)
        hidden = (jax.nn.silu(gate_vals) * up_vals).astype(jnp.bfloat16)
        partial_rows = jnp.dot(hidden, down_mat, preferred_element_type=jnp.float32).astype(
            jnp.bfloat16
        )
        return partial_rows.reshape(received.shape)

    def skip_rows(received):
        return jnp.zeros(received.shape, jnp.bfloat16)

    def run_experts(outgoing, active):
        received = lax.all_to_all(outgoing, "expert", split_axis=0, concat_axis=0, tiled=True)
        computed = lax.cond(active, expert_rows, skip_rows, received)
        returned = lax.all_to_all(computed, "expert", split_axis=0, concat_axis=0, tiled=True)
        return returned

    def advance(tick_count, carry):
        incoming, states = carry
        micro_at = tick_count - section_at
        active = (micro_at >= 0) & (micro_at < micro_count)
        micro_index = jnp.clip(micro_at, 0, micro_count - 1)
        fresh_rows = lax.dynamic_index_in_dim(tokens, micro_index, 0, keepdims=False)
        route_now = lax.dynamic_index_in_dim(route_all, micro_index, 0, keepdims=False)
        slot_now = lax.dynamic_index_in_dim(slot_all, micro_index, 0, keepdims=False)
        drop_now = lax.dynamic_index_in_dim(drop_all, micro_index, 0, keepdims=False)
        weigh_now = lax.dynamic_index_in_dim(weigh_all, micro_index, 0, keepdims=False)
        kept_mask = drop_now == 0
        passed_state = incoming[0]
        prior_rows = [incoming[1], incoming[2]]
        current = jnp.where(section_at == 0, fresh_rows, passed_state)
        wide_rows = current.astype(jnp.float32)
        inv_scale = lax.rsqrt(jnp.mean(wide_rows * wide_rows, axis=-1, keepdims=True) + 1e-05)
        normed = (wide_rows * inv_scale * gain_row).astype(jnp.bfloat16)
        local_id = route_now - half_at * local_count
        owned = kept_mask & (local_id >= 0) & (local_id < local_count)
        target = jnp.where(owned, local_id * capacity + slot_now, slot_limit)
        buffer = jnp.zeros((slot_limit, model_width), jnp.bfloat16)
        buffer = buffer.at[target[:, 0]].set(normed, mode="drop")
        buffer = buffer.at[target[:, 1]].set(normed, mode="drop")
        buffer = buffer.reshape(local_count, capacity, model_width)
        outgoing = jnp.repeat(buffer, shards, axis=0)
        returned = run_experts(outgoing, active)
        summed = jnp.sum(
            returned.astype(jnp.float32).reshape(local_count, shards, capacity, model_width), axis=1
        )
        flat_back = summed.astype(jnp.bfloat16).reshape(slot_limit, model_width)
        clipped = jnp.minimum(target, slot_limit - 1)
        combined = wide_rows
        chosen_rows = []
        for member in range(2):
            own_rows = flat_back[clipped[:, member]]
            chosen = jnp.where(owned[:, member : member + 1], own_rows, prior_rows[member])
            chosen_rows.append(chosen)
            combined = combined + weigh_now[:, member : member + 1] * chosen.astype(jnp.float32)
        mixed_rows = combined.astype(jnp.bfloat16)
        updated = lax.dynamic_update_index_in_dim(states, mixed_rows, micro_index, 0)
        states = jnp.where(active, updated, states)
        zero_rows = jnp.zeros_like(current)
        even_load = jnp.stack([current, chosen_rows[0], chosen_rows[1]])
        odd_load = jnp.stack([mixed_rows, zero_rows, zero_rows])
        payload = jnp.where(odd_section, odd_load, even_load)
        passed = shifted(shortened(payload), "section", 1).astype(payload.dtype)
        return (passed, states)

    start_load = jnp.zeros((3, tok_rows, model_width), jnp.bfloat16)
    initial = (start_load, jnp.zeros((micro_count, tok_rows, model_width), jnp.bfloat16))
    final_load, states = lax.fori_loop(0, micro_count + sections - 1, advance, initial)
    return states[None]


def solution(mesh):
    return jax.shard_map(
        on_device,
        mesh=mesh,
        in_specs=(
            P(None, "expert", None),
            P(),
            P("section", None, "expert"),
            P("section", None, "expert"),
            P("section", "expert", None),
            P(None, None, "expert", None),
            P(None, None, "expert", None),
            P(None, None, "expert", None),
            P(None, None, "expert", None),
        ),
        out_specs=P("section", None, "expert", None),
        check_vma=False,
    )
```

profile of v0, /device:TPU:4, one launch (start us, length us, event | category | flops | bytes accessed | tf_op | source)
XLA Modules:
  0.0 559.6 jit_solution(8104722328637122049)
XLA Ops:
  2.2 556.7 %while.17 = (s32[]{:T(128)}, bf16[3,8,2048]{2,1,0:T(8,128)(2,1)S(1)}, bf16[8,8,2048]{2,1,0:T(8,128)(2,1)S(1)}, pred[]{:T(512)}, pred[]{:T(512)}, /*index=5*/s32[...) while((s32[]{:T(128)}, ...), condition=%wide.region_7.8_spmd, body=%wide.region_0.7_spmd.sunk | while | flops 881903936 | bytes 27046772 | solution.py:109
  10.4 9.7 %all-to-all-done = bf16[8,5,2048]{2,1,0:T(8,128)(2,1)S(1)} async-done(((bf16[8,5,2048]{2,1,0:T(8,128)(2,1)}), bf16[8,5,2048]{2,1,0:T(8,128)(2,1)S(1)}, u32[]{:S(2)}, u32[]{:S(2)}) %all-to-all-start) | async-done | bytes 163872 | tf_op jit(solution)/shard_map/while/body/eval_jaxpr/all_to_all | solution.py:54
  24.3 9.6 %all-to-all-done.1 = bf16[8,5,2048]{2,1,0:T(8,128)(2,1)S(1)} async-done(((bf16[8,5,2048]{2,1,0:T(8,128)(2,1)}), bf16[8,5,2048]{2,1,0:T(8,128)(2,1)S(1)}, u32[]{:S(2)}, u32[]{:S(2)}) %all-to-all-start.1) | async-done | bytes 163872 | tf_op jit(solution)/shard_map/while/body/eval_jaxpr/all_to_all | solution.py:56
  63.2 9.6 %all-to-all-done.1 = bf16[8,5,2048]{2,1,0:T(8,128)(2,1)S(1)} async-done(((bf16[8,5,2048]{2,1,0:T(8,128)(2,1)}), bf16[8,5,2048]{2,1,0:T(8,128)(2,1)S(1)}, u32[]{:S(2)}, u32[]{:S(2)}) %all-to-all-start.1) | async-done | bytes 163872 | tf_op jit(solution)/shard_map/while/body/eval_jaxpr/all_to_all | solution.py:56
  76.7 25.1 %collective-permute-done = bf16[3,8,2048]{2,1,0:T(8,128)(2,1)S(1)} collective-permute-done((bf16[3,8,2048]{2,1,0:T(8,128)(2,1)S(1)}, bf16[3,8,2048]{2,1,0:T(8,128)(2,1)S(1)}, u32[]{:S(2)}, u32[]{:S(2)}) %collective-permute-start) | collective-permute-done | bytes 98336 | tf_op jit(solution)/shard_map/while/body/eval_jaxpr/ppermute | solution.py:16
  118.1 13.1 %conditional.2 = (bf16[8,5,2048]{2,1,0:T(8,128)(2,1)}) conditional(s32[]{:T(128)} %convert_element_type.138, () %tuple.73, (bf16[8,5,2048]{2,1,0:T(8,128)(2,1)S(1)}, bf16[2048,1792]{1,0:T(8,128)(2,1)}, bf16[2048,1792]{1,0:T(8,128)(2,1)}, bf16[1792,2048]{1,0:T(8,128)(2,1)}) %tuple.74), branch_computations={%region_4.4_spmd, %region_5.5_spmd} | conditional | flops 881315840 | bytes 23740424 | solution.py:55
  134.7 9.6 %all-to-all-done.1 = bf16[8,5,2048]{2,1,0:T(8,128)(2,1)S(1)} async-done(((bf16[8,5,2048]{2,1,0:T(8,128)(2,1)}), bf16[8,5,2048]{2,1,0:T(8,128)(2,1)S(1)}, u32[]{:S(2)}, u32[]{:S(2)}) %all-to-all-start.1) | async-done | bytes 163872 | tf_op jit(solution)/shard_map/while/body/eval_jaxpr/all_to_all | solution.py:56
  169.4 13.1 %conditional.2 = (bf16[8,5,2048]{2,1,0:T(8,128)(2,1)}) conditional(s32[]{:T(128)} %convert_element_type.138, () %tuple.73, (bf16[8,5,2048]{2,1,0:T(8,128)(2,1)S(1)}, bf16[2048,1792]{1,0:T(8,128)(2,1)}, bf16[2048,1792]{1,0:T(8,128)(2,1)}, bf16[1792,2048]{1,0:T(8,128)(2,1)}) %tuple.74), branch_computations={%region_4.4_spmd, %region_5.5_spmd} | conditional | flops 881315840 | bytes 23740424 | solution.py:55
  185.9 9.6 %all-to-all-done.1 = bf16[8,5,2048]{2,1,0:T(8,128)(2,1)S(1)} async-done(((bf16[8,5,2048]{2,1,0:T(8,128)(2,1)}), bf16[8,5,2048]{2,1,0:T(8,128)(2,1)S(1)}, u32[]{:S(2)}, u32[]{:S(2)}) %all-to-all-start.1) | async-done | bytes 163872 | tf_op jit(solution)/shard_map/while/body/eval_jaxpr/all_to_all | solution.py:56
  211.1 9.6 %all-to-all-done = bf16[8,5,2048]{2,1,0:T(8,128)(2,1)S(1)} async-done(((bf16[8,5,2048]{2,1,0:T(8,128)(2,1)}), bf16[8,5,2048]{2,1,0:T(8,128)(2,1)S(1)}, u32[]{:S(2)}, u32[]{:S(2)}) %all-to-all-start) | async-done | bytes 163872 | tf_op jit(solution)/shard_map/while/body/eval_jaxpr/all_to_all | solution.py:54
  220.6 13.1 %conditional.2 = (bf16[8,5,2048]{2,1,0:T(8,128)(2,1)}) conditional(s32[]{:T(128)} %convert_element_type.138, () %tuple.73, (bf16[8,5,2048]{2,1,0:T(8,128)(2,1)S(1)}, bf16[2048,1792]{1,0:T(8,128)(2,1)}, bf16[2048,1792]{1,0:T(8,128)(2,1)}, bf16[1792,2048]{1,0:T(8,128)(2,1)}) %tuple.74), branch_computations={%region_4.4_spmd, %region_5.5_spmd} | conditional | flops 881315840 | bytes 23740424 | solution.py:55
  237.2 9.6 %all-to-all-done.1 = bf16[8,5,2048]{2,1,0:T(8,128)(2,1)S(1)} async-done(((bf16[8,5,2048]{2,1,0:T(8,128)(2,1)}), bf16[8,5,2048]{2,1,0:T(8,128)(2,1)S(1)}, u32[]{:S(2)}, u32[]{:S(2)}) %all-to-all-start.1) | async-done | bytes 163872 | tf_op jit(solution)/shard_map/while/body/eval_jaxpr/all_to_all | solution.py:56
  271.9 13.1 %conditional.2 = (bf16[8,5,2048]{2,1,0:T(8,128)(2,1)}) conditional(s32[]{:T(128)} %convert_element_type.138, () %tuple.73, (bf16[8,5,2048]{2,1,0:T(8,128)(2,1)S(1)}, bf16[2048,1792]{1,0:T(8,128)(2,1)}, bf16[2048,1792]{1,0:T(8,128)(2,1)}, bf16[1792,2048]{1,0:T(8,128)(2,1)}) %tuple.74), branch_computations={%region_4.4_spmd, %region_5.5_spmd} | conditional | flops 881315840 | bytes 23740424 | solution.py:55
  288.4 9.6 %all-to-all-done.1 = bf16[8,5,2048]{2,1,0:T(8,128)(2,1)S(1)} async-done(((bf16[8,5,2048]{2,1,0:T(8,128)(2,1)}), bf16[8,5,2048]{2,1,0:T(8,128)(2,1)S(1)}, u32[]{:S(2)}, u32[]{:S(2)}) %all-to-all-start.1) | async-done | bytes 163872 | tf_op jit(solution)/shard_map/while/body/eval_jaxpr/all_to_all | solution.py:56
  323.1 13.1 %conditional.2 = (bf16[8,5,2048]{2,1,0:T(8,128)(2,1)}) conditional(s32[]{:T(128)} %convert_element_type.138, () %tuple.73, (bf16[8,5,2048]{2,1,0:T(8,128)(2,1)S(1)}, bf16[2048,1792]{1,0:T(8,128)(2,1)}, bf16[2048,1792]{1,0:T(8,128)(2,1)}, bf16[1792,2048]{1,0:T(8,128)(2,1)}) %tuple.74), branch_computations={%region_4.4_spmd, %region_5.5_spmd} | conditional | flops 881315840 | bytes 23740424 | solution.py:55
  339.7 9.6 %all-to-all-done.1 = bf16[8,5,2048]{2,1,0:T(8,128)(2,1)S(1)} async-done(((bf16[8,5,2048]{2,1,0:T(8,128)(2,1)}), bf16[8,5,2048]{2,1,0:T(8,128)(2,1)S(1)}, u32[]{:S(2)}, u32[]{:S(2)}) %all-to-all-start.1) | async-done | bytes 163872 | tf_op jit(solution)/shard_map/while/body/eval_jaxpr/all_to_all | solution.py:56
  374.4 13.1 %conditional.2 = (bf16[8,5,2048]{2,1,0:T(8,128)(2,1)}) conditional(s32[]{:T(128)} %convert_element_type.138, () %tuple.73, (bf16[8,5,2048]{2,1,0:T(8,128)(2,1)S(1)}, bf16[2048,1792]{1,0:T(8,128)(2,1)}, bf16[2048,1792]{1,0:T(8,128)(2,1)}, bf16[1792,2048]{1,0:T(8,128)(2,1)}) %tuple.74), branch_computations={%region_4.4_spmd, %region_5.5_spmd} | conditional | flops 881315840 | bytes 23740424 | solution.py:55
  390.9 9.6 %all-to-all-done.1 = bf16[8,5,2048]{2,1,0:T(8,128)(2,1)S(1)} async-done(((bf16[8,5,2048]{2,1,0:T(8,128)(2,1)}), bf16[8,5,2048]{2,1,0:T(8,128)(2,1)S(1)}, u32[]{:S(2)}, u32[]{:S(2)}) %all-to-all-start.1) | async-done | bytes 163872 | tf_op jit(solution)/shard_map/while/body/eval_jaxpr/all_to_all | solution.py:56
  425.7 13.1 %conditional.2 = (bf16[8,5,2048]{2,1,0:T(8,128)(2,1)}) conditional(s32[]{:T(128)} %convert_element_type.138, () %tuple.73, (bf16[8,5,2048]{2,1,0:T(8,128)(2,1)S(1)}, bf16[2048,1792]{1,0:T(8,128)(2,1)}, bf16[2048,1792]{1,0:T(8,128)(2,1)}, bf16[1792,2048]{1,0:T(8,128)(2,1)}) %tuple.74), branch_computations={%region_4.4_spmd, %region_5.5_spmd} | conditional | flops 881315840 | bytes 23740424 | solution.py:55
  442.2 9.6 %all-to-all-done.1 = bf16[8,5,2048]{2,1,0:T(8,128)(2,1)S(1)} async-done(((bf16[8,5,2048]{2,1,0:T(8,128)(2,1)}), bf16[8,5,2048]{2,1,0:T(8,128)(2,1)S(1)}, u32[]{:S(2)}, u32[]{:S(2)}) %all-to-all-start.1) | async-done | bytes 163872 | tf_op jit(solution)/shard_map/while/body/eval_jaxpr/all_to_all | solution.py:56
  476.9 13.1 %conditional.2 = (bf16[8,5,2048]{2,1,0:T(8,128)(2,1)}) conditional(s32[]{:T(128)} %convert_element_type.138, () %tuple.73, (bf16[8,5,2048]{2,1,0:T(8,128)(2,1)S(1)}, bf16[2048,1792]{1,0:T(8,128)(2,1)}, bf16[2048,1792]{1,0:T(8,128)(2,1)}, bf16[1792,2048]{1,0:T(8,128)(2,1)}) %tuple.74), branch_computations={%region_4.4_spmd, %region_5.5_spmd} | conditional | flops 881315840 | bytes 23740424 | solution.py:55
  493.4 9.6 %all-to-all-done.1 = bf16[8,5,2048]{2,1,0:T(8,128)(2,1)S(1)} async-done(((bf16[8,5,2048]{2,1,0:T(8,128)(2,1)}), bf16[8,5,2048]{2,1,0:T(8,128)(2,1)S(1)}, u32[]{:S(2)}, u32[]{:S(2)}) %all-to-all-start.1) | async-done | bytes 163872 | tf_op jit(solution)/shard_map/while/body/eval_jaxpr/all_to_all | solution.py:56
  532.3 9.6 %all-to-all-done.1 = bf16[8,5,2048]{2,1,0:T(8,128)(2,1)S(1)} async-done(((bf16[8,5,2048]{2,1,0:T(8,128)(2,1)}), bf16[8,5,2048]{2,1,0:T(8,128)(2,1)S(1)}, u32[]{:S(2)}, u32[]{:S(2)}) %all-to-all-start.1) | async-done | bytes 163872 | tf_op jit(solution)/shard_map/while/body/eval_jaxpr/all_to_all | solution.py:56
  543.3 13.4 %collective-permute-start = (bf16[3,8,2048]{2,1,0:T(8,128)(2,1)S(1)}, bf16[3,8,2048]{2,1,0:T(8,128)(2,1)S(1)}, u32[]{:S(2)}, u32[]{:S(2)}) collective-permute-start(bf16[3,8,2048]{2,1,0:T(8,128)(2,1)S(1)} %maximum_select_fusion.2), channel_id=1, source_target_pairs={{0,8},{8,16},{16,24},{1,9},{9,17},{17,25},{2,10},{10,18},{18,26},{... | collective-permute-start | bytes 294920 | tf_op jit(solution)/shard_map/while/body/eval_jaxpr/ppermute | solution.py:16
  (345 shorter events, 396.4 us)
Async XLA Ops:
  5.5 14.6 %all-to-all-start = ((bf16[8,5,2048]{2,1,0:T(8,128)(2,1)}), bf16[8,5,2048]{2,1,0:T(8,128)(2,1)S(1)}, u32[]{:S(2)}, u32[]{:S(2)}) async-start(bf16[8,5,2048]{2,1,0:T(8,128)(2,1)} %bitcast.98), calls=%async_computation | async-start | bytes 524288 | tf_op jit(solution)/shard_map/while/body/eval_jaxpr/all_to_all | solution.py:54
  20.8 13.1 %all-to-all-start.1 = ((bf16[8,5,2048]{2,1,0:T(8,128)(2,1)}), bf16[8,5,2048]{2,1,0:T(8,128)(2,1)S(1)}, u32[]{:S(2)}, u32[]{:S(2)}) async-start(bf16[8,5,2048]{2,1,0:T(8,128)(2,1)} %get-tuple-element.654), calls=%async_computation.1 | async-start | bytes 524288 | tf_op jit(solution)/shard_map/while/body/eval_jaxpr/all_to_all | solution.py:56
  45.9 13.1 %all-to-all-start = ((bf16[8,5,2048]{2,1,0:T(8,128)(2,1)}), bf16[8,5,2048]{2,1,0:T(8,128)(2,1)S(1)}, u32[]{:S(2)}, u32[]{:S(2)}) async-start(bf16[8,5,2048]{2,1,0:T(8,128)(2,1)} %bitcast.98), calls=%async_computation | async-start | bytes 524288 | tf_op jit(solution)/shard_map/while/body/eval_jaxpr/all_to_all | solution.py:54
  59.7 13.1 %all-to-all-start.1 = ((bf16[8,5,2048]{2,1,0:T(8,128)(2,1)}), bf16[8,5,2048]{2,1,0:T(8,128)(2,1)S(1)}, u32[]{:S(2)}, u32[]{:S(2)}) async-start(bf16[8,5,2048]{2,1,0:T(8,128)(2,1)} %get-tuple-element.654), calls=%async_computation.1 | async-start | bytes 524288 | tf_op jit(solution)/shard_map/while/body/eval_jaxpr/all_to_all | solution.py:56
  74.2 27.7 %collective-permute-start = (bf16[3,8,2048]{2,1,0:T(8,128)(2,1)S(1)}, bf16[3,8,2048]{2,1,0:T(8,128)(2,1)S(1)}, u32[]{:S(2)}, u32[]{:S(2)}) collective-permute-start(bf16[3,8,2048]{2,1,0:T(8,128)(2,1)S(1)} %maximum_select_fusion.2), channel_id=1, source_target_pairs={{0,8},{8,16},{16,24},{1,9},{9,17},{17,25},{2,10},{10,18},{18,26},{... | collective-permute-start | bytes 294920 | tf_op jit(solution)/shard_map/while/body/eval_jaxpr/ppermute | solution.py:16
  105.1 13.1 %all-to-all-start = ((bf16[8,5,2048]{2,1,0:T(8,128)(2,1)}), bf16[8,5,2048]{2,1,0:T(8,128)(2,1)S(1)}, u32[]{:S(2)}, u32[]{:S(2)}) async-start(bf16[8,5,2048]{2,1,0:T(8,128)(2,1)} %bitcast.98), calls=%async_computation | async-start | bytes 524288 | tf_op jit(solution)/shard_map/while/body/eval_jaxpr/all_to_all | solution.py:54
  131.2 13.1 %all-to-all-start.1 = ((bf16[8,5,2048]{2,1,0:T(8,128)(2,1)}), bf16[8,5,2048]{2,1,0:T(8,128)(2,1)S(1)}, u32[]{:S(2)}, u32[]{:S(2)}) async-start(bf16[8,5,2048]{2,1,0:T(8,128)(2,1)} %get-tuple-element.654), calls=%async_computation.1 | async-start | bytes 524288 | tf_op jit(solution)/shard_map/while/body/eval_jaxpr/all_to_all | solution.py:56
  156.3 13.1 %all-to-all-start = ((bf16[8,5,2048]{2,1,0:T(8,128)(2,1)}), bf16[8,5,2048]{2,1,0:T(8,128)(2,1)S(1)}, u32[]{:S(2)}, u32[]{:S(2)}) async-start(bf16[8,5,2048]{2,1,0:T(8,128)(2,1)} %bitcast.98), calls=%async_computation | async-start | bytes 524288 | tf_op jit(solution)/shard_map/while/body/eval_jaxpr/all_to_all | solution.py:54
  182.5 13.1 %all-to-all-start.1 = ((bf16[8,5,2048]{2,1,0:T(8,128)(2,1)}), bf16[8,5,2048]{2,1,0:T(8,128)(2,1)S(1)}, u32[]{:S(2)}, u32[]{:S(2)}) async-start(bf16[8,5,2048]{2,1,0:T(8,128)(2,1)} %get-tuple-element.654), calls=%async_computation.1 | async-start | bytes 524288 | tf_op jit(solution)/shard_map/while/body/eval_jaxpr/all_to_all | solution.py:56
  207.6 13.1 %all-to-all-start = ((bf16[8,5,2048]{2,1,0:T(8,128)(2,1)}), bf16[8,5,2048]{2,1,0:T(8,128)(2,1)S(1)}, u32[]{:S(2)}, u32[]{:S(2)}) async-start(bf16[8,5,2048]{2,1,0:T(8,128)(2,1)} %bitcast.98), calls=%async_computation | async-start | bytes 524288 | tf_op jit(solution)/shard_map/while/body/eval_jaxpr/all_to_all | solution.py:54
  233.7 13.1 %all-to-all-start.1 = ((bf16[8,5,2048]{2,1,0:T(8,128)(2,1)}), bf16[8,5,2048]{2,1,0:T(8,128)(2,1)S(1)}, u32[]{:S(2)}, u32[]{:S(2)}) async-start(bf16[8,5,2048]{2,1,0:T(8,128)(2,1)} %get-tuple-element.654), calls=%async_computation.1 | async-start | bytes 524288 | tf_op jit(solution)/shard_map/while/body/eval_jaxpr/all_to_all | solution.py:56
  258.8 13.1 %all-to-all-start = ((bf16[8,5,2048]{2,1,0:T(8,128)(2,1)}), bf16[8,5,2048]{2,1,0:T(8,128)(2,1)S(1)}, u32[]{:S(2)}, u32[]{:S(2)}) async-start(bf16[8,5,2048]{2,1,0:T(8,128)(2,1)} %bitcast.98), calls=%async_computation | async-start | bytes 524288 | tf_op jit(solution)/shard_map/while/body/eval_jaxpr/all_to_all | solution.py:54
  285.0 13.1 %all-to-all-start.1 = ((bf16[8,5,2048]{2,1,0:T(8,128)(2,1)}), bf16[8,5,2048]{2,1,0:T(8,128)(2,1)S(1)}, u32[]{:S(2)}, u32[]{:S(2)}) async-start(bf16[8,5,2048]{2,1,0:T(8,128)(2,1)} %get-tuple-element.654), calls=%async_computation.1 | async-start | bytes 524288 | tf_op jit(solution)/shard_map/while/body/eval_jaxpr/all_to_all | solution.py:56
  310.1 13.1 %all-to-all-start = ((bf16[8,5,2048]{2,1,0:T(8,128)(2,1)}), bf16[8,5,2048]{2,1,0:T(8,128)(2,1)S(1)}, u32[]{:S(2)}, u32[]{:S(2)}) async-start(bf16[8,5,2048]{2,1,0:T(8,128)(2,1)} %bitcast.98), calls=%async_computation | async-start | bytes 524288 | tf_op jit(solution)/shard_map/while/body/eval_jaxpr/all_to_all | solution.py:54
  336.2 13.1 %all-to-all-start.1 = ((bf16[8,5,2048]{2,1,0:T(8,128)(2,1)}), bf16[8,5,2048]{2,1,0:T(8,128)(2,1)S(1)}, u32[]{:S(2)}, u32[]{:S(2)}) async-start(bf16[8,5,2048]{2,1,0:T(8,128)(2,1)} %get-tuple-element.654), calls=%async_computation.1 | async-start | bytes 524288 | tf_op jit(solution)/shard_map/while/body/eval_jaxpr/all_to_all | solution.py:56
  361.3 13.1 %all-to-all-start = ((bf16[8,5,2048]{2,1,0:T(8,128)(2,1)}), bf16[8,5,2048]{2,1,0:T(8,128)(2,1)S(1)}, u32[]{:S(2)}, u32[]{:S(2)}) async-start(bf16[8,5,2048]{2,1,0:T(8,128)(2,1)} %bitcast.98), calls=%async_computation | async-start | bytes 524288 | tf_op jit(solution)/shard_map/while/body/eval_jaxpr/all_to_all | solution.py:54
  387.5 13.1 %all-to-all-start.1 = ((bf16[8,5,2048]{2,1,0:T(8,128)(2,1)}), bf16[8,5,2048]{2,1,0:T(8,128)(2,1)S(1)}, u32[]{:S(2)}, u32[]{:S(2)}) async-start(bf16[8,5,2048]{2,1,0:T(8,128)(2,1)} %get-tuple-element.654), calls=%async_computation.1 | async-start | bytes 524288 | tf_op jit(solution)/shard_map/while/body/eval_jaxpr/all_to_all | solution.py:56
  412.6 13.1 %all-to-all-start = ((bf16[8,5,2048]{2,1,0:T(8,128)(2,1)}), bf16[8,5,2048]{2,1,0:T(8,128)(2,1)S(1)}, u32[]{:S(2)}, u32[]{:S(2)}) async-start(bf16[8,5,2048]{2,1,0:T(8,128)(2,1)} %bitcast.98), calls=%async_computation | async-start | bytes 524288 | tf_op jit(solution)/shard_map/while/body/eval_jaxpr/all_to_all | solution.py:54
  438.7 13.1 %all-to-all-start.1 = ((bf16[8,5,2048]{2,1,0:T(8,128)(2,1)}), bf16[8,5,2048]{2,1,0:T(8,128)(2,1)S(1)}, u32[]{:S(2)}, u32[]{:S(2)}) async-start(bf16[8,5,2048]{2,1,0:T(8,128)(2,1)} %get-tuple-element.654), calls=%async_computation.1 | async-start | bytes 524288 | tf_op jit(solution)/shard_map/while/body/eval_jaxpr/all_to_all | solution.py:56
  463.8 13.1 %all-to-all-start = ((bf16[8,5,2048]{2,1,0:T(8,128)(2,1)}), bf16[8,5,2048]{2,1,0:T(8,128)(2,1)S(1)}, u32[]{:S(2)}, u32[]{:S(2)}) async-start(bf16[8,5,2048]{2,1,0:T(8,128)(2,1)} %bitcast.98), calls=%async_computation | async-start | bytes 524288 | tf_op jit(solution)/shard_map/while/body/eval_jaxpr/all_to_all | solution.py:54
  490.0 13.1 %all-to-all-start.1 = ((bf16[8,5,2048]{2,1,0:T(8,128)(2,1)}), bf16[8,5,2048]{2,1,0:T(8,128)(2,1)S(1)}, u32[]{:S(2)}, u32[]{:S(2)}) async-start(bf16[8,5,2048]{2,1,0:T(8,128)(2,1)} %get-tuple-element.654), calls=%async_computation.1 | async-start | bytes 524288 | tf_op jit(solution)/shard_map/while/body/eval_jaxpr/all_to_all | solution.py:56
  515.1 13.1 %all-to-all-start = ((bf16[8,5,2048]{2,1,0:T(8,128)(2,1)}), bf16[8,5,2048]{2,1,0:T(8,128)(2,1)S(1)}, u32[]{:S(2)}, u32[]{:S(2)}) async-start(bf16[8,5,2048]{2,1,0:T(8,128)(2,1)} %bitcast.98), calls=%async_computation | async-start | bytes 524288 | tf_op jit(solution)/shard_map/while/body/eval_jaxpr/all_to_all | solution.py:54
  528.9 13.1 %all-to-all-start.1 = ((bf16[8,5,2048]{2,1,0:T(8,128)(2,1)}), bf16[8,5,2048]{2,1,0:T(8,128)(2,1)S(1)}, u32[]{:S(2)}, u32[]{:S(2)}) async-start(bf16[8,5,2048]{2,1,0:T(8,128)(2,1)} %get-tuple-element.654), calls=%async_computation.1 | async-start | bytes 524288 | tf_op jit(solution)/shard_map/while/body/eval_jaxpr/all_to_all | solution.py:56
  543.3 15.6 %collective-permute-start = (bf16[3,8,2048]{2,1,0:T(8,128)(2,1)S(1)}, bf16[3,8,2048]{2,1,0:T(8,128)(2,1)S(1)}, u32[]{:S(2)}, u32[]{:S(2)}) collective-permute-start(bf16[3,8,2048]{2,1,0:T(8,128)(2,1)S(1)} %maximum_select_fusion.2), channel_id=1, source_target_pairs={{0,8},{8,16},{16,24},{1,9},{9,17},{17,25},{2,10},{10,18},{18,26},{... | collective-permute-start | bytes 294920 | tf_op jit(solution)/shard_map/while/body/eval_jaxpr/ppermute | solution.py:16
  (11 other events, 69.5 us)
where the time goes:
time: 564 us; the launch traced here: 560 us
  waiting for transfers between devices  286 us (51%)
  starting transfers between devices  111 us (20%)
  matrix products  97.6 us (17%)
  local copies, waits for them, and re-layouts  33.4 us (6%)
  other arithmetic  29.3 us (5%)
    all_to_all x11, waiting for transfers between devices, run_experts(): lax.all_to_all(computed, 'expert', split_axis=0, concat_axis=0, tiled=True)  106 us
    all_to_all x11, waiting for transfers between devices, run_experts(): lax.all_to_all(outgoing, 'expert', split_axis=0, concat_axis=0, tiled=True)  105 us
    ppermute x11, waiting for transfers between devices, shifted(): return lax.ppermute(value, axis, pairs)  75.1 us
    dot_general x8, matrix products, expert_rows(): jnp.dot(hidden, down_mat, preferred_element_type=jnp.float32)  62.1 us
    all_to_all x11, starting transfers between devices, run_experts(): lax.all_to_all(outgoing, 'expert', split_axis=0, concat_axis=0, tiled=True)  39 us
    all_to_all x11, starting transfers between devices, run_experts(): lax.all_to_all(computed, 'expert', split_axis=0, concat_axis=0, tiled=True)  37.5 us
    dot_general x8, matrix products, expert_rows(): gate_vals = jnp.dot(flat_rows, gate_mat, preferred_element_type=jnp.float32)  35.5 us
    ppermute x11, starting transfers between devices, shifted(): return lax.ppermute(value, axis, pairs)  34.7 us
  transfers between devices with their start and end apart: 33, of which 33 were waited for; matrix products, arithmetic and copies ran while one was open for 0% of the time, Pallas kernels for 0%

commit v1 on v0

v1 whole, which is shorter than its diff:
```python
import jax
import jax.numpy as jnp
from jax import lax
from jax.sharding import PartitionSpec as P


def on_device(tokens, norm_gain, w_gate, w_up, w_down, expert_ids, slot_ids, dropped, gate_weights):
    groups = lax.axis_size("expert")
    sections = lax.axis_size("section")
    section_at = lax.axis_index("section")
    layers = sections // 2
    local_count = 2
    experts = 2 * local_count
    shards = groups // local_count
    micro_count, tok_rows, model_width = tokens.shape
    capacity = 5 * tok_rows // (2 * experts)
    layer_at = section_at // 2
    half_at = section_at % 2
    gate_mat, up_mat, down_mat = w_gate[0], w_up[0], w_down[0]

    def own_layer(value):
        return lax.dynamic_index_in_dim(value, layer_at, 0, keepdims=False)

    gain_row = own_layer(norm_gain)
    local_id = own_layer(expert_ids) - half_at * local_count
    slot = own_layer(slot_ids)
    owned = (own_layer(dropped) == 0) & (local_id >= 0) & (local_id < local_count)
    weigh = own_layer(gate_weights)
    position = jnp.where(owned, local_id * capacity + slot, -1)
    hot = position[..., None] == jnp.arange(local_count * capacity)
    place = jnp.any(hot, axis=2).astype(jnp.bfloat16)
    spread = jnp.sum(jnp.where(hot, weigh[..., None], 0.0), axis=2)

    def expert_rows(received):
        flat = received.reshape(-1, model_width)
        gate_vals = jnp.dot(flat, gate_mat, preferred_element_type=jnp.float32)
        up_vals = jnp.dot(flat, up_mat, preferred_element_type=jnp.float32)
        hidden = (jax.nn.silu(gate_vals) * up_vals).astype(jnp.bfloat16)
        out = jnp.dot(hidden, down_mat, preferred_element_type=jnp.float32).astype(jnp.bfloat16)
        return out.reshape(received.shape)

    current = tokens
    states = jnp.zeros_like(tokens)
    for layer in range(layers):
        mine = layer_at == layer
        wide = current.astype(jnp.float32)
        inv = lax.rsqrt(jnp.mean(wide * wide, axis=-1, keepdims=True) + 1e-05)
        normed = (wide * inv * gain_row).astype(jnp.bfloat16)
        rows = jnp.einsum("mts,mtd->msd", place, normed, preferred_element_type=jnp.float32)
        rows = rows.astype(jnp.bfloat16).reshape(micro_count, local_count, capacity, model_width)
        rows = jnp.transpose(rows, (1, 0, 2, 3)).reshape(local_count, -1, model_width)
        received = lax.all_to_all(jnp.repeat(rows, shards, axis=0), "expert", 0, 0, tiled=True)
        computed = lax.cond(mine, expert_rows, jnp.zeros_like, received)
        returned = lax.all_to_all(computed, "expert", 0, 0, tiled=True)
        summed = jnp.sum(
            returned.astype(jnp.float32).reshape(local_count, shards, micro_count, capacity, model_width), axis=1
        )
        summed = jnp.transpose(summed.astype(jnp.bfloat16), (1, 0, 2, 3)).reshape(micro_count, -1, model_width)
        share = jnp.einsum(
            "mts,msd->mtd", spread, summed.astype(jnp.float32), precision=lax.Precision.HIGHEST
        )
        pairs = [(2 * layer, 2 * layer + 1), (2 * layer + 1, 2 * layer)]
        other = lax.ppermute(share.astype(jnp.bfloat16), "section", pairs)
        full = (wide + share + other.astype(jnp.float32)).astype(jnp.bfloat16)
        half = (wide + share).astype(jnp.bfloat16)
        states = jnp.where(mine, jnp.where(half_at == 0, half, full), states)
        if layer + 1 < layers:
            onward = [(2 * layer + i, 2 * layer + 2 + i) for i in range(2)]
            passed = lax.ppermute(full, "section", onward)
            current = jnp.where(layer_at == layer + 1, passed, current)
    return states[None]


def solution(mesh):
    return jax.shard_map(
        on_device,
        mesh=mesh,
        in_specs=(
            P(None, "expert", None),
            P(),
            P("section", None, "expert"),
            P("section", None, "expert"),
            P("section", "expert", None),
            P(None, None, "expert", None),
            P(None, None, "expert", None),
            P(None, None, "expert", None),
            P(None, None, "expert", None),
        ),
        out_specs=P("section", None, "expert", None),
        check_vma=False,
    )
```

time: 564 us -> 221 us (0.39)
  waiting for transfers between devices: 286 us -> 135 us
  starting transfers between devices: 111 us -> 17.5 us
  matrix products: 97.6 us -> 21.5 us
  blocking collectives: 0 us -> 34.6 us
  other arithmetic: 29.3 us -> 2.91 us
  local copies, waits for them, and re-layouts: 33.4 us -> 8.32 us
    all_to_all x22 -> x3, waiting for transfers between devices: 211 us -> 96.3 us  [the longest x2 64.4 us: on_device(): lax.all_to_all(jnp.repeat(rows, shards, axis=0), 'expert', 0, 0, tiled=True)]
    all_to_all x22 -> x3, starting transfers between devices: 76.5 us -> 12.2 us  [the longest x2 8.46 us: on_device(): lax.all_to_all(jnp.repeat(rows, shards, axis=0), 'expert', 0, 0, tiled=True)]
    dot_general x8 -> x1, matrix products: 62.1 us -> 11.8 us  [expert_rows(): jnp.dot(hidden, down_mat, preferred_element_type=jnp.float32)]
    ppermute x11 -> x3, waiting for transfers between devices: 75.1 us -> 39.2 us  [the longest x1 33 us: on_device(): passed = lax.ppermute(full, 'section', onward)]
    all_to_all x0 -> x1, blocking collectives: none -> 34.6 us  [on_device(): returned = lax.all_to_all(computed, 'expert', 0, 0, tiled=True)]
    ppermute x11 -> x3, starting transfers between devices: 34.7 us -> 5.36 us  [the longest x2 4.07 us: on_device(): other = lax.ppermute(share.astype(jnp.bfloat16), 'section', pairs)]
    dot_general x8 -> x5, matrix products: 35.5 us -> 9.68 us  [the longest x1 7.03 us: expert_rows(): gate_vals = jnp.dot(flat, gate_mat, preferred_element_type=jnp.float32)]
    scatter x22 -> x0, other arithmetic: 16.9 us -> none  [the longest x11 8.7 us: advance(): buffer = buffer.at[target[:, 1]].set(normed, mode='drop')]
  transfers between devices with their start and end apart: 33 -> 6, of which waited for: 33 -> 5; matrix products, arithmetic and copies ran while one was open for 0% -> 0% of each run, Pallas kernels for 0% -> 0%
where the time goes in v1:
time: 221 us
  waiting for transfers between devices  135 us (61%)
  blocking collectives  34.6 us (16%)
  matrix products  21.5 us (10%)
  starting transfers between devices  17.5 us (8%)
  local copies, waits for them, and re-layouts  8.32 us (4%)
  other arithmetic  2.91 us (1%)
    all_to_all x2, waiting for transfers between devices, on_device(): lax.all_to_all(jnp.repeat(rows, shards, axis=0), 'expert', 0, 0, tiled=True)  64.4 us
    all_to_all x1, blocking collectives, on_device(): returned = lax.all_to_all(computed, 'expert', 0, 0, tiled=True)  34.6 us
    ppermute x1, waiting for transfers between devices, on_device(): passed = lax.ppermute(full, 'section', onward)  33 us
    all_to_all x1, waiting for transfers between devices, on_device(): returned = lax.all_to_all(computed, 'expert', 0, 0, tiled=True)  31.9 us
    dot_general x1, matrix products, expert_rows(): jnp.dot(hidden, down_mat, preferred_element_type=jnp.float32)  11.8 us
    all_to_all x2, starting transfers between devices, on_device(): lax.all_to_all(jnp.repeat(rows, shards, axis=0), 'expert', 0, 0, tiled=True)  8.46 us
    dot_general x1, matrix products, expert_rows(): gate_vals = jnp.dot(flat, gate_mat, preferred_element_type=jnp.float32)  7.03 us
    ppermute x2, waiting for transfers between devices, on_device(): other = lax.ppermute(share.astype(jnp.bfloat16), 'section', pairs)  6.17 us
  transfers between devices with their start and end apart: 6, of which 5 were waited for; matrix products, arithmetic and copies ran while one was open for 0% of the time, Pallas kernels for 0%

profile of v1, /device:TPU:4, one launch (start us, length us, event | category | flops | bytes accessed | tf_op | source)
XLA Modules:
  0.0 220.6 jit_solution(16269420209216900204)
XLA Ops:
  0.0 1.1 fusion.4
  1.1 0.7 constant_dynamic-slice_fusion.4
  1.8 0.7 constant_dynamic-slice_fusion.2
  2.7 1.3 convolution_convert_fusion.3
  4.6 1.2 broadcast_in_dim.41
  5.8 4.9 %all-to-all-start = ((bf16[8,40,2048]{2,1,0:T(8,128)(2,1)}), bf16[8,40,2048]{2,1,0:T(8,128)(2,1)S(1)}, u32[]{:S(2)}, u32[]{:S(2)}) async-start(bf16[8,40,2048]{2,1,0:T(8,128)(2,1)} %bitcast.10), calls=%async_computation | async-start | bytes 2621440 | tf_op jit(solution)/shard_map/all_to_all | solution.py:52
  10.7 32.2 %all-to-all-done = bf16[8,40,2048]{2,1,0:T(8,128)(2,1)S(1)} async-done(((bf16[8,40,2048]{2,1,0:T(8,128)(2,1)}), bf16[8,40,2048]{2,1,0:T(8,128)(2,1)S(1)}, u32[]{:S(2)}, u32[]{:S(2)}) %all-to-all-start) | async-done | bytes 1310752 | tf_op jit(solution)/shard_map/all_to_all | solution.py:52
  42.9 1.2 conditional.2
  42.9 1.2 broadcast.71
  44.1 3.7 %all-to-all-start.1 = ((bf16[8,40,2048]{2,1,0:T(8,128)(2,1)}), bf16[8,40,2048]{2,1,0:T(8,128)(2,1)S(1)}, u32[]{:S(2)}, u32[]{:S(2)}) async-start(bf16[8,40,2048]{2,1,0:T(8,128)(2,1)} %get-tuple-element.41), calls=%async_computation.1 | async-start | bytes 2621440 | tf_op jit(solution)/shard_map/all_to_all | solution.py:54
  48.0 31.9 %all-to-all-done.1 = bf16[8,40,2048]{2,1,0:T(8,128)(2,1)S(1)} async-done(((bf16[8,40,2048]{2,1,0:T(8,128)(2,1)}), bf16[8,40,2048]{2,1,0:T(8,128)(2,1)S(1)}, u32[]{:S(2)}, u32[]{:S(2)}) %all-to-all-start.1) | async-done | bytes 1310752 | tf_op jit(solution)/shard_map/all_to_all | solution.py:54
  81.9 1.3 collective-permute-start.1
  83.2 33.0 %collective-permute-done.1 = bf16[8,8,2048]{2,1,0:T(8,128)(2,1)S(1)} collective-permute-done((bf16[8,8,2048]{2,1,0:T(8,128)(2,1)S(1)}, bf16[8,8,2048]{2,1,0:T(8,128)(2,1)S(1)}, u32[]{:S(2)}, u32[]{:S(2)}) %collective-permute-start.1) | collective-permute-done | bytes 262176 | tf_op jit(solution)/shard_map/ppermute | solution.py:69
  117.4 1.2 broadcast_in_dim.42
  118.6 3.6 %all-to-all-start.2 = ((bf16[8,40,2048]{2,1,0:T(8,128)(2,1)}), bf16[8,40,2048]{2,1,0:T(8,128)(2,1)S(1)}, u32[]{:S(2)}, u32[]{:S(2)}) async-start(bf16[8,40,2048]{2,1,0:T(8,128)(2,1)} %bitcast.21), calls=%async_computation.2 | async-start | bytes 2621440 | tf_op jit(solution)/shard_map/all_to_all | solution.py:52
  122.2 32.2 %all-to-all-done.2 = bf16[8,40,2048]{2,1,0:T(8,128)(2,1)S(1)} async-done(((bf16[8,40,2048]{2,1,0:T(8,128)(2,1)}), bf16[8,40,2048]{2,1,0:T(8,128)(2,1)S(1)}, u32[]{:S(2)}, u32[]{:S(2)}) %all-to-all-start.2) | async-done | bytes 1310752 | tf_op jit(solution)/shard_map/all_to_all | solution.py:52
  154.4 19.9 %conditional.3 = (bf16[8,40,2048]{2,1,0:T(8,128)(2,1)S(1)}) conditional(s32[]{:T(128)} %convert_element_type.89, () %tuple.19, (bf16[8,40,2048]{2,1,0:T(8,128)(2,1)S(1)}, bf16[2048,1792]{1,0:T(8,128)(2,1)}, bf16[2048,1792]{1,0:T(8,128)(2,1)}, bf16[1792,2048]{1,0:T(8,128)(2,1)}) %tuple.33), branch_computations={%region_7.8_spmd, %region_8.9_spmd} | conditional | flops 7050526720 | bytes 35782692 | solution.py:53
  154.4 1.1 copy-done.2
  155.4 7.0 %fusion.35 = f32[320,1792]{1,0:T(8,128)} fusion(bf16[320,2048]{1,0:T(8,128)(2,1)S(1)} %bitcast.56, bf16[2048,1792]{1,0:T(8,128)(2,1)} %get-tuple-element.32), kind=kOutput, calls=%fused_computation.63 | convolution fusion | flops 2348810240 | bytes 10944512 | tf_op jit(solution)/shard_map/cond/branch_1_fun/dot_general | solution.py:36
  162.5 11.8 %convolution_convert_fusion.1 = bf16[320,2048]{1,0:T(8,128)(2,1)S(1)} fusion(bf16[1792,2048]{1,0:T(8,128)(2,1)} %get-tuple-element.34, bf16[320,2048]{1,0:T(8,128)(2,1)} %bitcast.57, bf16[2048,1792]{1,0:T(8,128)(2,1)} %get-tuple-element.33, f32[320,1792]{1,0:T(8,128)} %fusion.35), kind=kOutput, calls=%fused_computation.6 | convolution fusion | flops 4701716480 | bytes 19595264 | tf_op jit(solution)/shard_map/cond/branch_1_fun/dot_general | solution.py:39
  174.3 34.6 %all_to_all.20 = bf16[8,40,2048]{2,1,0:T(8,128)(2,1)S(1)} all-to-all(bf16[8,40,2048]{2,1,0:T(8,128)(2,1)S(1)} %get-tuple-element.42), channel_id=1, replica_groups=mesh['section'=4,'expert'=8] {'expert'}, dimensions={0} | all-to-all | bytes 2621440 | tf_op jit(solution)/shard_map/all_to_all | solution.py:54
  210.1 3.4 %collective-permute-start.2 = (bf16[8,8,2048]{2,1,0:T(8,128)(2,1)S(1)}, bf16[8,8,2048]{2,1,0:T(8,128)(2,1)S(1)}, u32[]{:S(2)}, u32[]{:S(2)}) collective-permute-start(bf16[8,8,2048]{2,1,0:T(8,128)(2,1)S(1)} %get-tuple-element.37), channel_id=1, source_target_pairs={{16,24},{24,16},{17,25},{25,17},{18,26},{26,18},{19,27},{27,19},{2... | collective-permute-start | bytes 786440 | tf_op jit(solution)/shard_map/ppermute | solution.py:63
  213.5 6.2 %collective-permute-done.2 = bf16[8,8,2048]{2,1,0:T(8,128)(2,1)S(1)} collective-permute-done((bf16[8,8,2048]{2,1,0:T(8,128)(2,1)S(1)}, bf16[8,8,2048]{2,1,0:T(8,128)(2,1)S(1)}, u32[]{:S(2)}, u32[]{:S(2)}) %collective-permute-start.2) | collective-permute-done | bytes 262176 | tf_op jit(solution)/shard_map/ppermute | solution.py:63
  219.6 0.9 fusion.18
  (36 shorter events, 5.1 us)
Async XLA Ops:
  0.0 1.1 copy-start
  5.8 37.1 %all-to-all-start = ((bf16[8,40,2048]{2,1,0:T(8,128)(2,1)}), bf16[8,40,2048]{2,1,0:T(8,128)(2,1)S(1)}, u32[]{:S(2)}, u32[]{:S(2)}) async-start(bf16[8,40,2048]{2,1,0:T(8,128)(2,1)} %bitcast.10), calls=%async_computation | async-start | bytes 2621440 | tf_op jit(solution)/shard_map/all_to_all | solution.py:52
  44.1 3.7 %copy-start.3 = (f32[2,8,8,2]{2,3,1,0:T(2,128)S(1)}, f32[2,8,8,2]{2,3,1,0:T(2,128)}, u32[]{:S(2)}) copy-start(f32[2,8,8,2]{2,3,1,0:T(2,128)} %param.21) | copy-start | bytes 3076
  44.1 35.8 %all-to-all-start.1 = ((bf16[8,40,2048]{2,1,0:T(8,128)(2,1)}), bf16[8,40,2048]{2,1,0:T(8,128)(2,1)S(1)}, u32[]{:S(2)}, u32[]{:S(2)}) async-start(bf16[8,40,2048]{2,1,0:T(8,128)(2,1)} %get-tuple-element.41), calls=%async_computation.1 | async-start | bytes 2621440 | tf_op jit(solution)/shard_map/all_to_all | solution.py:54
  47.8 33.9 %copy-start.1 = (bf16[8,8,2048]{2,1,0:T(8,128)(2,1)S(1)}, bf16[8,8,2048]{2,1,0:T(8,128)(2,1)}, u32[]{:S(2)}) copy-start(bf16[8,8,2048]{2,1,0:T(8,128)(2,1)} %param.13) | copy-start | bytes 786436
  81.1 0.7 collective-permute-start
  81.9 34.3 %collective-permute-start.1 = (bf16[8,8,2048]{2,1,0:T(8,128)(2,1)S(1)}, bf16[8,8,2048]{2,1,0:T(8,128)(2,1)S(1)}, u32[]{:S(2)}, u32[]{:S(2)}) collective-permute-start(bf16[8,8,2048]{2,1,0:T(8,128)(2,1)S(1)} %add_convert_fusion.1), channel_id=1, source_target_pairs={{0,16},{8,24},{1,17},{9,25},{2,18},{10,26},{3,19},{11,27},{4,20},{... | collective-permute-start | bytes 786440 | tf_op jit(solution)/shard_map/ppermute | solution.py:69
  118.6 35.8 %all-to-all-start.2 = ((bf16[8,40,2048]{2,1,0:T(8,128)(2,1)}), bf16[8,40,2048]{2,1,0:T(8,128)(2,1)S(1)}, u32[]{:S(2)}, u32[]{:S(2)}) async-start(bf16[8,40,2048]{2,1,0:T(8,128)(2,1)} %bitcast.21), calls=%async_computation.2 | async-start | bytes 2621440 | tf_op jit(solution)/shard_map/all_to_all | solution.py:52
  154.4 1.1 copy-start.2
  210.1 9.6 %collective-permute-start.2 = (bf16[8,8,2048]{2,1,0:T(8,128)(2,1)S(1)}, bf16[8,8,2048]{2,1,0:T(8,128)(2,1)S(1)}, u32[]{:S(2)}, u32[]{:S(2)}) collective-permute-start(bf16[8,8,2048]{2,1,0:T(8,128)(2,1)S(1)} %get-tuple-element.37), channel_id=1, source_target_pairs={{16,24},{24,16},{17,25},{25,17},{18,26},{26,18},{19,27},{27,19},{2... | collective-permute-start | bytes 786440 | tf_op jit(solution)/shard_map/ppermute | solution.py:63

commit v2 on v1

v2 whole, which is shorter than its diff:
```python
import functools

import jax
import jax.numpy as jnp
from jax import lax
from jax.experimental import pallas as pl
from jax.experimental.pallas import tpu as pltpu
from jax.sharding import PartitionSpec as P

CORES = 2
TILE_ROWS = 16


def kernel(
    groups, layers, chunks, rows,
    tok, gain, pos_row, pos_col, weigh, gate_hbm, up_hbm, down_hbm,
    out,
    gate, up, down, rbuf, sbuf, pbuf, twin, rsum, retbuf, share_out, share_in, fbuf, xin, hid,
    wsem, disp_send, disp_recv, relay_send, twin_send, twin_recv, ret_send, ret_recv,
    share_send, share_recv, x_send, x_recv,
):
    chips = groups // CORES
    per_expert = chips // 2
    model_width = tok.shape[-1]
    width = gate.shape[-1]
    section = lax.axis_index("section")
    me = lax.axis_index("expert")
    layer = section // 2
    half = section % 2
    chip = me // CORES
    core = me % CORES
    sibling = me + 1 - 2 * core
    partner = section + 1 - 2 * half

    def fetch(i):
        src, dst = ((gate_hbm, gate), (up_hbm, up), (down_hbm, down))[i]
        return pltpu.make_async_copy(src.at[0], dst, wsem.at[i])

    def span(index, count=1):
        size = rows * count
        return pl.ds(pl.multiple_of(index * size, TILE_ROWS), size)

    def remote(src, dst, send, recv, **where):
        return pltpu.make_async_remote_copy(
            src_ref=src, dst_ref=dst, send_sem=send, recv_sem=recv,
            device_id=where, device_id_type=pl.DeviceIdType.MESH,
        )

    def chip_at(r):
        return lax.rem(chip + r, chips)

    def direct(c, r):
        there = chip_at(r)
        place = span(core * chips + chip)
        return remote(
            sbuf.at[c, span(there // per_expert)], rbuf.at[c, place], disp_send.at[c, r],
            disp_recv.at[c, core * chips + chip], expert=there * CORES + core,
        )

    def own_rows(c):
        place = core * chips + chip
        return remote(
            sbuf.at[c, span(chip // per_expert)], rbuf.at[c, span(place)], disp_send.at[c, 0],
            disp_recv.at[c, place], expert=sibling,
        )

    def relay(c, r):
        place = core * chips + chip_at(r)
        return remote(
            rbuf.at[c, span(place)], rbuf.at[c, span(place)], relay_send.at[c, r],
            disp_recv.at[c, place], expert=sibling,
        )

    def arrival(c, at_core, at_chip):
        place = at_core * chips + at_chip
        return remote(
            rbuf.at[c, span(place)], rbuf.at[c, span(place)], relay_send.at[c, 0],
            disp_recv.at[c, place], expert=sibling,
        )

    def to_twin(c):
        return remote(
            pbuf.at[c, span(1 - core, chips)], twin.at[c], twin_send.at[c], twin_recv.at[c], expert=sibling
        )

    def giving(c, r):
        there = chip_at(r)
        return remote(
            rsum.at[c, span(there)], retbuf.at[c, span(chip)], ret_send.at[c, r], ret_recv.at[c, chip],
            expert=there * CORES + core,
        )

    def given(c, r):
        there = chip_at(r)
        return remote(
            rsum.at[c, span(there)], retbuf.at[c, span(there)], ret_send.at[c, r], ret_recv.at[c, there],
            expert=there * CORES + core,
        )

    def swap(c):
        return remote(share_out.at[c], share_in.at[c], share_send.at[c], share_recv.at[c], section=partner)

    def hand_on(c):
        return remote(fbuf.at[c], xin.at[c], x_send.at[c], x_recv.at[c], section=lax.rem(section + 2, 2 * layers))

    def dispatch(c):
        current = xin[c].astype(jnp.float32)
        inv = lax.rsqrt(jnp.mean(current * current, axis=-1, keepdims=True) + 1e-05)
        normed = (current * inv * gain[...]).astype(jnp.bfloat16)
        slots = lax.broadcasted_iota(jnp.int32, (2 * rows, tok.shape[1]), 0)
        hot = (slots == pos_row[c, 0:1, :]) | (slots == pos_row[c, 1:2, :])
        place = jnp.where(hot, 1.0, 0.0).astype(jnp.bfloat16)
        sent = jnp.dot(place, normed, preferred_element_type=jnp.float32).astype(jnp.bfloat16)
        sbuf[c] = sent
        own = jnp.where(chip // per_expert == 0, sent[:rows], sent[rows:])
        rbuf[c, span(core * chips + chip), :] = own
        for r in range(chips - 1, 0, -1):
            direct(c, r).start()
        own_rows(c).start()

    def forward(c):
        for r in range(1, chips):
            arrival(c, core, chip_at(r)).wait_recv()
            relay(c, r).start()

    def compute(c):
        for r in range(chips):
            arrival(c, 1 - core, chip_at(r)).wait_recv()
        if c == 0:
            fetch(0).wait()
            fetch(1).wait()
        wide = 256 if width % 256 == 0 else 128

        def inner(t, carry):
            cols = pl.ds(pl.multiple_of(t * wide, wide), wide)
            got = rbuf[c]
            g = jnp.dot(got, gate[:, cols], preferred_element_type=jnp.float32)
            u = jnp.dot(got, up[:, cols], preferred_element_type=jnp.float32)
            hid[:, cols] = (g / (1.0 + jnp.exp(-g)) * u).astype(jnp.bfloat16)
            return carry

        lax.fori_loop(0, width // wide, inner, 0)
        if c == 0:
            fetch(2).wait()

        def outer(t, carry):
            cols = pl.ds(pl.multiple_of(t * 256, 256), 256)
            pbuf[c, :, cols] = jnp.dot(hid[...], down[:, cols], preferred_element_type=jnp.float32).astype(
                jnp.bfloat16
            )
            return carry

        lax.fori_loop(0, model_width // 256, outer, 0)
        to_twin(c).start()

    def pair(c):
        to_twin(c).wait_recv()
        mine = pbuf[c, span(core, chips), :].astype(jnp.float32)
        rsum[c] = (mine + twin[c].astype(jnp.float32)).astype(jnp.bfloat16)
        for r in range(chips - 1, 0, -1):
            giving(c, r).start()
        retbuf[c, span(chip), :] = rsum[c, span(chip), :]

    def combine(c):
        for r in range(1, chips):
            given(c, r).wait_recv()
        parts = []
        for j in range(2):
            total = jnp.zeros((rows, model_width), jnp.float32)
            for i in range(per_expert):
                low = (j * per_expert + i) * rows
                total = total + retbuf[c, low : low + rows, :].astype(jnp.float32)
            parts.append(total)
        made = jnp.concatenate(parts, axis=0)
        slots = lax.broadcasted_iota(jnp.int32, (tok.shape[1], 2 * rows), 1)
        spread = jnp.zeros((tok.shape[1], 2 * rows), jnp.float32)
        for k in range(2):
            spread = spread + jnp.where(slots == pos_col[c, :, k : k + 1], weigh[c, :, k : k + 1], 0.0)
        share = jnp.dot(spread, made, precision=lax.Precision.HIGHEST, preferred_element_type=jnp.float32)
        share_out[c] = share.astype(jnp.bfloat16)
        swap(c).start()
        out[c] = (xin[c].astype(jnp.float32) + share).astype(jnp.bfloat16)

    def finish(c):
        swap(c).wait_recv()
        both = share_out[c].astype(jnp.float32) + share_in[c].astype(jnp.float32)
        full = (xin[c].astype(jnp.float32) + both).astype(jnp.bfloat16)
        fbuf[c] = full

        @pl.when(layer < layers - 1)
        def _():
            hand_on(c).start()

        @pl.when(half == 1)
        def _():
            out[c] = full

    @pl.when(layer == 0)
    def _():
        for c in range(chunks):
            xin[c] = tok[c]
            dispatch(c)

    for i in range(3):
        fetch(i).start()

    def later(c):
        if c < chunks:
            @pl.when(layer > 0)
            def _():
                hand_on(c).wait_recv()
                dispatch(c)

    later(0)
    forward(0)
    for c in range(chunks):
        compute(c)
        pair(c)
        later(c + 1)
        if c + 1 < chunks:
            forward(c + 1)
        if c >= 1:
            finish(c - 1)
        combine(c)
    finish(chunks - 1)

    for c in range(chunks):
        own_rows(c).wait_send()
        to_twin(c).wait_send()
        swap(c).wait_send()
        for r in range(1, chips):
            direct(c, r).wait_send()
            relay(c, r).wait_send()
            giving(c, r).wait_send()

    @pl.when(layer < layers - 1)
    def _():
        for c in range(chunks):
            hand_on(c).wait_send()


def on_device(tokens, norm_gain, w_gate, w_up, w_down, expert_ids, slot_ids, dropped, gate_weights):
    groups = lax.axis_size("expert")
    layers = lax.axis_size("section") // 2
    section_at = lax.axis_index("section")
    local_count = 2
    micro_count, tok_rows, model_width = tokens.shape
    width = w_gate.shape[-1]
    capacity = 5 * tok_rows // (4 * local_count)
    layer_at, half_at = section_at // 2, section_at % 2
    per_chunk = max(1, TILE_ROWS // capacity)
    rows = -(-per_chunk * capacity // TILE_ROWS) * TILE_ROWS
    chunks = -(-micro_count // per_chunk)
    held = per_chunk * tok_rows
    lines = -(-held // TILE_ROWS) * TILE_ROWS
    chips = groups // CORES

    def chunked(value, fill):
        rest = value.shape[2:]
        extra = [(0, chunks * per_chunk - micro_count)] + [(0, 0)] * (value.ndim - 1)
        value = jnp.pad(value, extra, constant_values=fill).reshape((chunks, held) + rest)
        return jnp.pad(value, [(0, 0), (0, lines - held)] + [(0, 0)] * len(rest), constant_values=fill)

    def own_layer(value):
        return lax.dynamic_index_in_dim(value, layer_at, 0, keepdims=False)

    local_id = own_layer(expert_ids) - half_at * local_count
    owned = (own_layer(dropped) == 0) & (local_id >= 0) & (local_id < local_count)
    turn = (jnp.arange(micro_count, dtype=jnp.int32) % per_chunk)[:, None, None]
    position = jnp.where(owned, local_id * rows + turn * capacity + own_layer(slot_ids), -1)
    pos_col = chunked(position, -1)
    pos_row = jnp.transpose(pos_col, (0, 2, 1))
    weigh = chunked(own_layer(gate_weights), 0)
    gain_row = lax.dynamic_slice_in_dim(norm_gain, layer_at, 1, 0)

    vm = pl.BlockSpec(memory_space=pltpu.VMEM)
    hb = pl.BlockSpec(memory_space=pl.ANY)
    half16 = jnp.bfloat16
    dma = pltpu.SemaphoreType.DMA
    made = pl.pallas_call(
        functools.partial(kernel, groups, layers, chunks, rows),
        out_shape=jax.ShapeDtypeStruct((chunks, lines, model_width), half16),
        in_specs=[vm] * 5 + [hb] * 3,
        out_specs=vm,
        scratch_shapes=[
            pltpu.VMEM((model_width, width), half16),
            pltpu.VMEM((model_width, width), half16),
            pltpu.VMEM((width, model_width), half16),
            pltpu.VMEM((chunks, groups * rows, model_width), half16),
            pltpu.VMEM((chunks, 2 * rows, model_width), half16),
            pltpu.VMEM((chunks, groups * rows, model_width), half16),
            pltpu.VMEM((chunks, chips * rows, model_width), half16),
            pltpu.VMEM((chunks, chips * rows, model_width), half16),
            pltpu.VMEM((chunks, chips * rows, model_width), half16),
            pltpu.VMEM((chunks, lines, model_width), half16),
            pltpu.VMEM((chunks, lines, model_width), half16),
            pltpu.VMEM((chunks, lines, model_width), half16),
            pltpu.VMEM((chunks, lines, model_width), half16),
            pltpu.VMEM((groups * rows, width), half16),
            dma((3,)),
            dma((chunks, chips)),
            dma((chunks, groups)),
            dma((chunks, chips)),
            dma((chunks,)),
            dma((chunks,)),
            dma((chunks, chips)),
            dma((chunks, chips)),
            dma((chunks,)),
            dma((chunks,)),
            dma((chunks,)),
            dma((chunks,)),
        ],
        compiler_params=pltpu.CompilerParams(has_side_effects=True, vmem_limit_bytes=58 * 1024 * 1024),
    )(chunked(tokens, 0), gain_row, pos_row, pos_col, weigh, w_gate, w_up, w_down)
    made = made[:, :held].reshape(chunks * per_chunk, tok_rows, model_width)
    return made[None, :micro_count]


def solution(mesh):
    return jax.shard_map(
        on_device,
        mesh=mesh,
        in_specs=(
            P(None, "expert", None),
            P(),
            P("section", None, "expert"),
            P("section", None, "expert"),
            P("section", "expert", None),
            P(None, None, "expert", None),
            P(None, None, "expert", None),
            P(None, None, "expert", None),
            P(None, None, "expert", None),
        ),
        out_specs=P("section", None, "expert", None),
        check_vma=False,
    )
```

time: 221 us -> 125 us (0.57)
  waiting for transfers between devices: 135 us -> 0 us
  Pallas kernels: 0 us -> 115 us
  blocking collectives: 34.6 us -> 0 us
  matrix products: 21.5 us -> 0 us
  starting transfers between devices: 17.5 us -> 0 us
  other arithmetic: 2.91 us -> 0.08 us
    pallas_call x0 -> x1, Pallas kernels: none -> 115 us  [on_device(): pl.pallas_call(functools.partial(kernel, groups, layers, chunks, rows), o...]
    all_to_all x3 -> x0, waiting for transfers between devices: 96.3 us -> none  [the longest x2 64.4 us: on_device(): lax.all_to_all(jnp.repeat(rows, shards, axis=0), 'expert', 0, 0, tiled=True)]
    ppermute x3 -> x0, waiting for transfers between devices: 39.2 us -> none  [the longest x1 33 us: on_device(): passed = lax.ppermute(full, 'section', onward)]
    all_to_all x1 -> x0, blocking collectives: 34.6 us -> none  [on_device(): returned = lax.all_to_all(computed, 'expert', 0, 0, tiled=True)]
    dot_general x6 -> x0, matrix products: 21.5 us -> none  [the longest x1 11.8 us: expert_rows(): jnp.dot(hidden, down_mat, preferred_element_type=jnp.float32)]
    all_to_all x3 -> x0, starting transfers between devices: 12.2 us -> none  [the longest x2 8.46 us: on_device(): lax.all_to_all(jnp.repeat(rows, shards, axis=0), 'expert', 0, 0, tiled=True)]
    ppermute x3 -> x0, starting transfers between devices: 5.36 us -> none  [the longest x2 4.07 us: on_device(): other = lax.ppermute(share.astype(jnp.bfloat16), 'section', pairs)]
    pad x0 -> x6, local copies, waits for them, and re-layouts: none -> 3.02 us  [the longest x3 2.04 us: chunked(): jnp.pad(value, [(0, 0), (0, lines - held)] + [(0, 0)] * len(rest), consta...]
  transfers between devices with their start and end apart: 6 -> 0, of which waited for: 5 -> 0; matrix products, arithmetic and copies ran while one was open for 0% -> 0% of each run, Pallas kernels for 0% -> 0%
where the time goes in v2:
time: 125 us; the launch traced here: 124 us
  Pallas kernels  115 us (92%)
  local copies, waits for them, and re-layouts  9.07 us (7%)
    pallas_call x1, Pallas kernels, on_device(): pl.pallas_call(functools.partial(kernel, groups, layers, chunks, rows), o...  115 us

profile of v2, /device:TPU:4, one launch (start us, length us, event | category | flops | bytes accessed | tf_op | source)
XLA Modules:
  0.0 124.4 jit_solution(10227827976585658725)
XLA Ops:
  0.0 0.0 copy-start
  0.0 0.7 copy-done
  0.7 0.6 constant_dynamic-slice_fusion.4.gain
  1.3 0.7 constant_dynamic-slice_fusion.3
  2.0 0.7 constant_dynamic-slice_fusion
  2.7 0.7 constant_dynamic-slice_fusion.1
  3.4 0.1 fusion.1
  3.5 0.1 copy.21
  3.6 0.1 copy.23
  3.8 0.6 pad.29.weigh
  4.4 0.6 fusion.6
  5.0 0.7 copy.16.pos_row
  5.7 1.0 pad.24
  6.7 0.8 pad.25.tok
  7.5 115.2 %shard_map.91 = bf16[3,32,2048]{2,1,0:T(8,128)(2,1)} custom-call(bf16[3,32,2048]{2,1,0:T(8,128)(2,1)} %pad.25.tok, f32[1,2048]{1,0:T(1,128)} %constant_dynamic-slice_fusion.4.gain, s32[3,2,32]{2,1,0:T(2,128)} %copy.16.pos_row, s32[3,32,2]{2,1,0:T(8,128)} %get-tuple-element.5.pos_col, f32[3,32,2]{2,1,0:T(8,128)} %pad.29.weigh, ...), custom_call_target="tpu_custom_call" | custom-call | tf_op jit(solution)/shard_map/pallas_call | solution.py:280
  122.7 1.0 slice.6
  123.7 0.7 slice_bitcast_fusion
  (3 shorter events, 0.0 us)
Async XLA Ops:
  0.0 0.7 copy-start

commit v3 on v2

--- a/solution.py
+++ b/solution.py
@@ -139,18 +139,18 @@
             hid[:, cols] = (g / (1.0 + jnp.exp(-g)) * u).astype(jnp.bfloat16)
             return carry
 
-        lax.fori_loop(0, width // wide, inner, 0)
+        lax.fori_loop(0, width // wide, inner, 0, unroll=True)
         if c == 0:
             fetch(2).wait()
 
         def outer(t, carry):
-            cols = pl.ds(pl.multiple_of(t * 256, 256), 256)
+            cols = pl.ds(pl.multiple_of(t * 512, 512), 512)
             pbuf[c, :, cols] = jnp.dot(hid[...], down[:, cols], preferred_element_type=jnp.float32).astype(
                 jnp.bfloat16
             )
             return carry
 
-        lax.fori_loop(0, model_width // 256, outer, 0)
+        lax.fori_loop(0, model_width // 512, outer, 0)
         to_twin(c).start()
 
     def pair(c):
@@ -195,14 +195,12 @@
         def _():
             out[c] = full
 
-    @pl.when(layer == 0)
-    def _():
-        for c in range(chunks):
-            xin[c] = tok[c]
-            dispatch(c)
-
-    for i in range(3):
-        fetch(i).start()
+    def first(c):
+        if c < chunks:
+            @pl.when(layer == 0)
+            def _():
+                xin[c] = tok[c]
+                dispatch(c)
 
     def later(c):
         if c < chunks:
@@ -211,17 +209,24 @@
                 hand_on(c).wait_recv()
                 dispatch(c)
 
+    first(0)
+    first(1)
+    for i in range(3):
+        fetch(i).start()
     later(0)
     forward(0)
     for c in range(chunks):
         compute(c)
         pair(c)
+        first(c + 2)
         later(c + 1)
+        if c >= 1:
+            combine(c - 1)
         if c + 1 < chunks:
             forward(c + 1)
         if c >= 1:
             finish(c - 1)
-        combine(c)
+    combine(chunks - 1)
     finish(chunks - 1)
 
     for c in range(chunks):

time: 125 us -> 115 us (0.920)
  Pallas kernels: 115 us -> 105 us
    pallas_call x1, Pallas kernels: 115 us -> 105 us  [on_device(): pl.pallas_call(functools.partial(kernel, groups, layers, chunks, rows), o...]
where the time goes in v3:
time: 115 us; the launch traced here: 114 us
  Pallas kernels  105 us (91%)
  local copies, waits for them, and re-layouts  9.07 us (8%)
    pallas_call x1, Pallas kernels, on_device(): pl.pallas_call(functools.partial(kernel, groups, layers, chunks, rows), o...  105 us

profile of v3, /device:TPU:4, one launch (start us, length us, event | category | flops | bytes accessed | tf_op | source)
XLA Modules:
  0.0 114.4 jit_solution(7487567516334428703)
XLA Ops:
  0.0 0.0 copy-start
  0.0 0.7 copy-done
  0.7 0.6 constant_dynamic-slice_fusion.4.gain
  1.3 0.7 constant_dynamic-slice_fusion.3
  2.0 0.7 constant_dynamic-slice_fusion
  2.7 0.7 constant_dynamic-slice_fusion.1
  3.4 0.1 fusion.1
  3.5 0.1 copy.21
  3.6 0.1 copy.23
  3.8 0.6 pad.29.weigh
  4.4 0.6 fusion.6
  5.0 0.7 copy.16.pos_row
  5.7 1.0 pad.24
  6.7 0.8 pad.25.tok
  7.5 105.2 %shard_map.91 = bf16[3,32,2048]{2,1,0:T(8,128)(2,1)} custom-call(bf16[3,32,2048]{2,1,0:T(8,128)(2,1)} %pad.25.tok, f32[1,2048]{1,0:T(1,128)} %constant_dynamic-slice_fusion.4.gain, s32[3,2,32]{2,1,0:T(2,128)} %copy.16.pos_row, s32[3,32,2]{2,1,0:T(8,128)} %get-tuple-element.5.pos_col, f32[3,32,2]{2,1,0:T(8,128)} %pad.29.weigh, ...), custom_call_target="tpu_custom_call" | custom-call | tf_op jit(solution)/shard_map/pallas_call | solution.py:285
  112.7 1.0 slice.6
  113.7 0.7 slice_bitcast_fusion
  (3 shorter events, 0.0 us)
Async XLA Ops:
  0.0 0.7 copy-start
